TPU v7x, 32 devices: a whole 2x2x4 slice. The times are simulated.
32 devices in a mesh: row: 8 (over z, y), col: 4 (over x, core).
Axes of the slice: x: 2, y: 2, z: 4, core: 2. Of those that a mesh axis runs over, the one named last changes fastest.
Arguments:
- interior_factor: float32 [8, 4, 1, 384, 384], P('row', 'col'), as said below
- coupling_in: bfloat16 [8, 4, 1, 384, 2048], P('row', 'col'), may hold values from -1.5 to 1.5
- coupling_back: bfloat16 [8, 4, 1, 384, 2048], P('row', 'col'), may hold values from -1.5 to 1.5
- interface_block: bfloat16 [8, 4, 1, 2048, 2048], P('row', 'col'), may hold values from -6 to 6
- gran_count: int32 [8, 4, 1], replicated, may hold values from 2 to 16, as said below
- gran_index: int32 [8, 4, 1, 16], replicated, may hold values from 0 to 15, as said below
Outputs:
- schur: float32 [8, 3, 1024, 1024], P('row', None, 'col')
Inputs may be any that keep to these rules, and one draw needn't show every extreme that they name: `gran_count`: each entry is an even number of granules; in every row group some subdomain has 16. `gran_index`: each row is an order of the 16 window granules, each once; window granule p of row group r is global granule 8 * r + p modulo 8 * 8; the first gran_count entries are the subdomain's interface granules. `interior_factor`: lower triangular with a positive diagonal.
All inputs are finite; a program needn't handle non-finite values.
Results may differ from a plain program's by a relative error of at most 0.0003.
Values may be sent and summed in bfloat16 or wider, within the bound.
A program may use at most 128 MiB of HBM per device.

v0:
```python
import jax
import jax.numpy as jnp
from jax import lax
from jax.sharding import PartitionSpec as P


def from_behind(block, axis, distance):
    devices = range(lax.axis_size(axis))
    route = [((i - distance) % len(devices), i) for i in devices]
    return lax.ppermute(block, axis, route)


def select_table(count, index):
    slots = jnp.arange(index.shape[0], dtype=jnp.int32)
    live = (slots < count).astype(jnp.float32)
    return (index[:, None] == slots[None, :]).astype(jnp.float32) * live[:, None]


def place(local, table):
    wing = table.shape[0]
    width = local.shape[0]
    granule = width // wing
    blocks = local.reshape(wing, granule, wing, granule)
    moved = jnp.einsum("ap,aibj,bq->piqj", table, blocks, table, precision=lax.Precision.HIGHEST)
    return moved.reshape(width, width)


def solve_columns(factor, coupling, block_count, block):
    height, width = coupling.shape

    def solve_block(block_no, total):
        piece = lax.dynamic_slice_in_dim(coupling, block_no * block, block, 1).astype(jnp.float32)
        solved = lax.linalg.triangular_solve(factor, piece, left_side=True, lower=True)
        return lax.dynamic_update_slice_in_dim(total, solved, block_no * block, 1)

    solved = lax.fori_loop(0, block_count, solve_block, jnp.zeros((height, width), jnp.float32))
    return solved.astype(jnp.bfloat16)


def schur_rows(solved_in, solved_back, block_count, block):
    width = solved_in.shape[1]

    def product_block(block_no, total):
        columns = lax.dynamic_slice_in_dim(solved_back, block_no * block, block, 1)
        rows_out = lax.dot_general(
            columns, solved_in, (((0,), (0,)), ((), ())), preferred_element_type=jnp.float32
        )
        return lax.dynamic_update_slice_in_dim(total, rows_out, block_no * block, 0)

    return lax.fori_loop(0, block_count, product_block, jnp.zeros((width, width), jnp.float32))


def on_device(interior_factor, coupling_in, coupling_back, interface_block, gran_count, gran_index):
    row_id = lax.axis_index("row")
    col_id = lax.axis_index("col")
    factors = interior_factor[0, 0]
    inputs = coupling_in[0, 0]
    backs = coupling_back[0, 0]
    own_blocks = interface_block[0, 0]
    width = inputs.shape[-1]
    wing = gran_index.shape[-1]
    granule = width // wing
    block = 2 * granule
    half = width // 2
    my_counts = gran_count[row_id, col_id]
    my_index = gran_index[row_id, col_id]
    my_blocks = my_counts // 2
    member = 0
    solved = [
        (
            solve_columns(factors[member], inputs[member], my_blocks[member], block),
            solve_columns(factors[member], backs[member], my_blocks[member], block),
        )
    ]
    member = 0
    product = schur_rows(solved[member][0], solved[member][1], my_blocks[member], block)
    local = own_blocks[member].astype(jnp.float32) - product
    window = place(local, select_table(my_counts[member], my_index[member]))
    quarters = jnp.stack(
        [window[:half, :half], window[:half, half:], window[half:, :half], window[half:, half:]]
    )
    summed = lax.psum_scatter(quarters, "col", scatter_dimension=1, tiled=True)
    carried = from_behind(summed[3], "row", 1)
    result = jnp.stack([summed[0] + carried, summed[1], summed[2]])
    return result[None]


def solution(mesh):
    in_specs = (
        P("row", "col", None, None, None),
        P("row", "col", None, None, None),
        P("row", "col", None, None, None),
        P("row", "col", None, None, None),
        P(),
        P(),
    )
    out_specs = P("row", None, "col", None)
    return jax.shard_map(
        on_device, mesh=mesh, in_specs=in_specs, out_specs=out_specs, check_vma=False
    )
```

profile of v0, /device:TPU:0, one launch (start us, length us, event | category | flops | bytes accessed | tf_op | source)
XLA Modules:
  0.0 941.6 jit_solution(15323263090492089952)
XLA Ops:
  6.5 1.2 constant_dynamic-slice_fusion.2
  10.4 0.7 compare_convert_fusion
  11.3 39.2 %while.37 = (s32[]{:T(128)}, bf16[384,2048]{1,0:T(8,128)(2,1)S(1)}, s32[]{:T(128)}, bf16[384,2048]{1,0:T(8,128)(2,1)}, f32[384,384]{1,0:T(8,128)}, /*index=5*/s3...) while((s32[]{:T(128)}, bf16[384,2048]{1,0:T(8,128)(2,1)S(1)}, s32[]{:T(128)}, ...), condition=%wide.region_1.3_spmd, body=%wide.region_0.2_spmd.sunk | while | flops 303104000 | bytes 4456816 | solution.py:36
  11.3 1.0 dynamic-slice_convert_fusion.4
  12.3 1.1 fusion.88
  13.4 6.0 while.41
  13.5 0.6 fusion.106
  14.1 1.3 bitcast_dynamic-update-slice_fusion.5
  15.5 0.6 fusion.106
  16.1 1.3 bitcast_dynamic-update-slice_fusion.5
  17.5 0.6 fusion.106
  18.1 1.3 bitcast_dynamic-update-slice_fusion.5
  19.4 29.5 %custom-call.13 = f32[3,128,128]{1,2,0:T(8,128)S(1)} custom-call(f32[3,128,128]{2,1,0:T(8,128)S(1)} %get-tuple-element.313), custom_call_target="InvertDiagBlocksLowerTriangular" | custom-call | tf_op jit(solution)/shard_map/while/body/triangular_solve/custom-call.1 | solution.py:33
  48.9 0.3 fusion.89
  49.5 0.3 fusion.90
  50.1 0.3 fusion.91
  50.5 1.1 copy-done.3
  51.8 39.2 %while.39 = (s32[]{:T(128)}, bf16[384,2048]{1,0:T(8,128)(2,1)S(1)}, s32[]{:T(128)}, bf16[384,2048]{1,0:T(8,128)(2,1)}, f32[384,384]{1,0:T(8,128)}, /*index=5*/s3...) while((s32[]{:T(128)}, bf16[384,2048]{1,0:T(8,128)(2,1)S(1)}, s32[]{:T(128)}, ...), condition=%wide.region_3.5_spmd, body=%wide.region_2.4_spmd.sunk | while | flops 303104000 | bytes 4456816 | solution.py:36
  51.9 1.0 dynamic-slice_convert_fusion.5
  52.8 1.1 fusion.99
  53.9 6.0 while.42
  54.0 0.6 fusion.105
  54.6 1.3 bitcast_dynamic-update-slice_fusion.4
  56.0 0.6 fusion.105
  56.6 1.3 bitcast_dynamic-update-slice_fusion.4
  58.0 0.6 fusion.105
  58.6 1.3 bitcast_dynamic-update-slice_fusion.4
  60.0 29.5 %custom-call.15 = f32[3,128,128]{1,2,0:T(8,128)S(1)} custom-call(f32[3,128,128]{2,1,0:T(8,128)S(1)} %get-tuple-element.320), custom_call_target="InvertDiagBlocksLowerTriangular" | custom-call | tf_op jit(solution)/shard_map/while/body/triangular_solve/custom-call.1 | solution.py:33
  89.5 0.3 fusion.100
  90.1 0.3 fusion.101
  90.4 0.3 convolution_subtract_fusion.11
  90.7 0.3 fusion.102
  91.0 7.9 broadcast_in_dim.8
  98.9 3.0 while.40
  98.9 3.0 convolution_dynamic-update-slice_fusion.2
  101.9 9.1 fusion.24
  111.0 7.5 copy.11
  118.5 32.3 %fusion.27 = f32[128,16,128,16]{2,3,1,0:T(8,128)} fusion(f32[16,128,16,128]{3,2,1,0:T(8,128)} %bitcast.120, f32[16]{0:T(128)S(1)} %compare_convert_fusion, s32[16]{0:T(128)S(1)} %dynamic-slice_bitcast_fusion), kind=kOutput, calls=%fused_computation.53 | convolution fusion | flops 805306880 | bytes 33554560 | tf_op jit(solution)/shard_map/ap,aibj,bq->piqj/dot_general | solution.py:24
  150.8 27.3 %fusion.29 = f32[16,128,16,128]{3,2,0,1:T(8,128)} fusion(f32[128,16,128,16]{2,3,1,0:T(8,128)} %fusion.27, f32[16]{0:T(128)S(1)} %compare_convert_fusion, s32[16]{0:T(128)S(1)} %dynamic-slice_bitcast_fusion), kind=kOutput, calls=%fused_computation.55 | convolution fusion | flops 805306880 | bytes 33554560 | tf_op jit(solution)/shard_map/ap,aibj,bq->piqj/dot_general | solution.py:24
  178.1 6.8 copy.7
  184.8 6.1 copy.20
  191.0 4.7 slice_bitcast_fusion.15
  195.7 10.7 %pad_maximum_fusion = f32[4,1024,1024]{2,1,0:T(8,128)} fusion(f32[1,1024,1024]{2,1,0:T(8,128)} %get-tuple-element.160, f32[1,1024,1024]{2,1,0:T(8,128)} %get-tuple-element.161, f32[1,1024,1024]{2,1,0:T(8,128)} %get-tuple-element.162, f32[1,1024,1024]{2,1,0:T(8,128)S(1)} %get-tuple-element.159), kind=kLoop, calls=%fused_computation.48 | loop fusion | flops 12582912 | bytes 33554432 | tf_op jit(solution)/shard_map/stack | solution.py:79
  206.4 696.8 %reduce-scatter.2.cloned.1.call-done = f32[4,256,1024]{2,1,0:T(8,128)} async-done(((f32[4,1024,1024]{2,1,0:T(8,128)}), f32[4,256,1024]{2,1,0:T(8,128)}) %reduce-scatter.2.cloned.1.call-update) | async-done | bytes 4194320 | tf_op jit(solution)/shard_map/reduce_scatter | solution.py:82
  903.2 1.4 slice_bitcast_fusion.16
  904.7 1.5 collective-permute-start
  906.2 26.0 %collective-permute-done = f32[256,1024]{1,0:T(8,128)S(1)} collective-permute-done((f32[256,1024]{1,0:T(8,128)S(1)}, f32[256,1024]{1,0:T(8,128)S(1)}, u32[]{:S(2)}, u32[]{:S(2)}) %collective-permute-start) | collective-permute-done | bytes 1048608 | tf_op jit(solution)/shard_map/ppermute | solution.py:10
  932.4 2.0 maximum_bitcast_fusion
  (32 shorter events, 1.9 us)
Async XLA Ops:
  6.5 3.9 copy-start
  6.5 896.7 %reduce-scatter.2.cloned.1.call-start = ((), (), s32[]{:S(2)}) async-start(), calls=%async_computation.1 | async-start | bytes 20971520 | tf_op jit(solution)/shard_map/reduce_scatter | solution.py:82
  50.5 1.1 copy-start.3
  903.2 29.0 %copy-start.2 = (f32[4,256,1024]{2,1,0:T(8,128)S(1)}, f32[4,256,1024]{2,1,0:T(8,128)}, u32[]{:S(2)}) copy-start(f32[4,256,1024]{2,1,0:T(8,128)} %reduce-scatter.2.cloned.1.call-done) | copy-start | bytes 12582916
  904.7 27.7 %slice-start = ((f32[4,256,1024]{2,1,0:T(8,128)}), f32[2,256,1024]{2,1,0:T(8,128)S(1)}, s32[]{:S(2)}) async-start(f32[4,256,1024]{2,1,0:T(8,128)} %reduce-scatter.2.cloned.1.call-done), calls=%async_computation.2 | async-start | bytes 4194304 | tf_op jit(solution)/shard_map/slice | solution.py:84
  904.7 27.5 %collective-permute-start = (f32[256,1024]{1,0:T(8,128)S(1)}, f32[256,1024]{1,0:T(8,128)S(1)}, u32[]{:S(2)}, u32[]{:S(2)}) collective-permute-start(f32[256,1024]{1,0:T(8,128)S(1)} %slice_bitcast_fusion.16), channel_id=1, source_target_pairs={{28,0},{0,4},{4,8},{8,12},{12,16},{16,20},{20,24},{24,28},{29,1},{... | collective-permute-start | bytes 3145736 | tf_op jit(solution)/shard_map/ppermute | solution.py:10
  906.2 28.2 %copy-start.1 = (s32[8,4,1,16]{3,2,1,0:T(1,128)S(1)}, s32[8,4,1,16]{3,2,1,0:T(1,128)}, u32[]{:S(2)}) copy-start(s32[8,4,1,16]{3,2,1,0:T(1,128)} %param.19) | copy-start | bytes 6148
Sparse Core Ops, SparseCore 0:
  206.5 696.6 reduce-scatter.1
where the time goes:
time: 956 us; the launch traced here: 942 us
  waiting for transfers between devices  723 us (76%)
  other arithmetic  85.8 us (9%)
  matrix products  65.5 us (7%)
  local copies, waits for them, and re-layouts  49.1 us (5%)
  between operations  16.5 us (2%)
    reduce_scatter x1, waiting for transfers between devices, on_device(): summed = lax.psum_scatter(quarters, 'col', scatter_dimension=1, tiled=True)  697 us
    another operation x8, other arithmetic, solve_block(): lax.linalg.triangular_solve(factor, piece, left_side=True, lower=True)  61.2 us
    dot_general x2, matrix products, place(): jnp.einsum('ap,aibj,bq->piqj', table, blocks, table, precision=lax.Precis...  59.6 us
    ppermute x1, waiting for transfers between devices, from_behind(): return lax.ppermute(block, axis, route)  26 us
  transfers between devices with their start and end apart: 2, of which 2 were waited for; matrix products, arithmetic and copies ran while one was open for 0% of the time, Pallas kernels for 0%

commit v1 on v0

v1 whole, which is shorter than its diff:
```python
import functools

import jax
import jax.numpy as jnp
from jax import lax
from jax.experimental import pallas as pl
from jax.experimental.pallas import tpu as pltpu
from jax.sharding import PartitionSpec as P

MESH = pl.DeviceIdType.MESH
HIGHEST = lax.Precision.HIGHEST


def exact_dot(a, b):
    return jnp.dot(a, b, precision=HIGHEST, preferred_element_type=jnp.float32)


def invert_tile(tile):
    size = tile.shape[0]
    i = lax.broadcasted_iota(jnp.int32, tile.shape, 0)
    j = lax.broadcasted_iota(jnp.int32, tile.shape, 1)
    inverse = jnp.where(i == j, 1.0 / jnp.where(i == j, tile, 1.0), 0.0)
    k = 1
    while k < size:
        both = 2 * k
        mask = (i // both == j // both) & (i % both >= k) & (j % both < k)
        below = jnp.where(mask, tile, 0.0)
        inverse = inverse - exact_dot(inverse, exact_dot(below, inverse))
        k = both
    return inverse


def invert_lower(factor_ref, tile, inverse_refs):
    count = factor_ref.shape[0] // tile
    at = lambda b: pl.ds(b * tile, tile)
    diagonal = [invert_tile(factor_ref[at(b), at(b)]) for b in range(count)]
    tiles = {}
    for col in range(count):
        tiles[col, col] = diagonal[col]
        for row in range(col + 1, count):
            total = exact_dot(factor_ref[at(row), at(col)], tiles[col, col])
            for mid in range(col + 1, row):
                total = total + exact_dot(factor_ref[at(row), at(mid)], tiles[mid, col])
            tiles[row, col] = -exact_dot(diagonal[row], total)
    for row in range(count):
        for col in range(count):
            rest = tiles[row, col] if col <= row else jnp.zeros((tile, tile), jnp.float32)
            for ref in inverse_refs:
                piece = rest.astype(jnp.bfloat16)
                ref[at(row), at(col)] = piece
                rest = rest - piece.astype(jnp.float32)


def assemble_kernel(
    granule, tile, slot_ref, live_ref, factor_ref, in_ref, back_ref, own_ref, out_ref,
    high_ref, mid_ref, low_ref, placed_in, placed_back,
):
    wing = placed_in.shape[1] // granule
    p = pl.program_id(0)

    def granule_of(ref, q):
        return ref[:, pl.ds(pl.multiple_of(slot_ref[q] * granule, granule), granule)]

    @pl.when(p == 0)
    def _():
        invert_lower(factor_ref, tile, (high_ref, mid_ref, low_ref))
        step = 4 if wing % 4 == 0 else 1
        for source, target in ((in_ref, placed_in), (back_ref, placed_back)):
            for first in range(0, wing, step):
                pieces = []
                for q in range(first, first + step):
                    piece = granule_of(source, q)
                    pieces.append(jnp.where(live_ref[q] == 1, piece, jnp.zeros_like(piece)))
                coupling = jnp.concatenate(pieces, axis=1) if step > 1 else pieces[0]
                solved = sum(
                    jnp.dot(ref[...], coupling, preferred_element_type=jnp.float32)
                    for ref in (low_ref, mid_ref, high_ref)
                )
                target[:, pl.ds(first * granule, step * granule)] = solved.astype(jnp.bfloat16)

    @pl.when(live_ref[p] == 1)
    def _():
        columns = placed_back[:, pl.ds(pl.multiple_of(p * granule, granule), granule)]
        product = lax.dot_general(
            columns, placed_in[...], (((0,), (0,)), ((), ())), preferred_element_type=jnp.float32
        )
        for q in range(wing):
            block = granule_of(own_ref, q).astype(jnp.float32)
            block = jnp.where(live_ref[q] == 1, block, 0.0)
            out_ref[:, q * granule:(q + 1) * granule] = (
                block - product[:, q * granule:(q + 1) * granule]
            )

    @pl.when(live_ref[p] != 1)
    def _():
        out_ref[...] = jnp.zeros_like(out_ref)


def assemble(slot, live, factor, inner, back, own):
    ni, width = inner.shape
    wing = slot.shape[0]
    granule = width // wing
    tile = 128 if ni % 128 == 0 else ni
    whole = lambda shape: pl.BlockSpec(shape, lambda p, s, l: (0, 0))
    return pl.pallas_call(
        functools.partial(assemble_kernel, granule, tile),
        grid_spec=pltpu.PrefetchScalarGridSpec(
            num_scalar_prefetch=2,
            grid=(wing,),
            in_specs=[
                whole((ni, ni)),
                whole((ni, width)),
                whole((ni, width)),
                pl.BlockSpec((granule, width), lambda p, s, l: (s[p], 0)),
            ],
            out_specs=pl.BlockSpec((granule, width), lambda p, s, l: (p, 0)),
            scratch_shapes=[pltpu.VMEM((ni, ni), jnp.bfloat16)] * 3
            + [pltpu.VMEM((ni, width), jnp.bfloat16)] * 2,
        ),
        out_shape=jax.ShapeDtypeStruct((width, width), jnp.float32),
        compiler_params=pltpu.CompilerParams(vmem_limit_bytes=40 * 2**20),
    )(slot, live, factor, inner, back, own)


def exchange_kernel(
    n_row, n_col, w_ref, out_ref,
    mine, paired, arrived, carried,
    load_sem, send1, recv1, send2, recv2, send3, recv3,
):
    chips = n_col // 2
    rows, half = mine.shape[2], mine.shape[3]
    r = lax.axis_index("row")
    c = lax.axis_index("col")
    chip, core = c // 2, c % 2
    partner = chip * 2 + (1 - core)
    after = lax.rem(r + 1, n_row)
    before = lax.rem(r + n_row - 1, n_row)

    barrier = pltpu.get_barrier_semaphore()
    greet = [(r, partner), (after, c), (before, c)]
    greet += [(r, lax.rem(chip + o, chips) * 2 + core) for o in range(1, chips)]
    for device in greet:
        pl.semaphore_signal(barrier, inc=1, device_id=device, device_id_type=MESH)

    order = [3, 2, 1, 0]
    offsets = list(range(1, chips)) + [0]

    def part(q, o, which):
        device = lax.rem(chip + o, chips) * 2 + which
        return w_ref.at[q // 2, device, :, pl.ds((q % 2) * half, half)]

    loads, first, second = {}, {}, {}
    for q in order:
        for o in offsets:
            loads[q, o] = pltpu.make_async_copy(part(q, o, core), mine.at[q, o], load_sem.at[q, o])
            loads[q, o].start()
    pl.semaphore_wait(barrier, len(greet))
    for q in order:
        for o in offsets:
            first[q, o] = pltpu.make_async_remote_copy(
                src_ref=part(q, o, 1 - core), dst_ref=paired.at[q, o],
                send_sem=send1.at[q, o], recv_sem=recv1.at[q, o],
                device_id=(r, partner), device_id_type=MESH,
            )
            first[q, o].start()
    for q in order:
        for o in offsets:
            loads[q, o].wait()
            first[q, o].wait_recv()
            mine[q, o] = mine[q, o] + paired[q, o]
            if o:
                device = lax.rem(chip + o, chips) * 2 + core
                second[q, o] = pltpu.make_async_remote_copy(
                    src_ref=mine.at[q, o], dst_ref=arrived.at[q, o - 1],
                    send_sem=send2.at[q, o - 1], recv_sem=recv2.at[q, o - 1],
                    device_id=(r, device), device_id_type=MESH,
                )
                second[q, o].start()
    carry = pltpu.make_async_remote_copy(
        src_ref=mine.at[3, 0], dst_ref=carried, send_sem=send3, recv_sem=recv3,
        device_id=(after, c), device_id_type=MESH,
    )
    for q in order:
        total = mine[q, 0]
        for o in range(1, chips):
            second[q, o].wait_recv()
            total = total + arrived[q, o - 1]
        if q == 3:
            mine[q, 0] = total
            carry.start()
        elif q > 0:
            out_ref[q] = total
        else:
            carry.wait_recv()
            out_ref[q] = total + carried[...]
    for copy in first.values():
        copy.wait_send()
    for copy in second.values():
        copy.wait_send()
    carry.wait_send()


def exchange(window, n_row, n_col):
    width = window.shape[-1]
    half = width // 2
    rows = half // n_col
    chips = n_col // 2
    dma = pltpu.SemaphoreType.DMA
    return pl.pallas_call(
        functools.partial(exchange_kernel, n_row, n_col),
        out_shape=jax.ShapeDtypeStruct((3, rows, half), jnp.float32),
        in_specs=[pl.BlockSpec(memory_space=pl.ANY)],
        out_specs=pl.BlockSpec(memory_space=pltpu.VMEM),
        scratch_shapes=[
            pltpu.VMEM((4, chips, rows, half), jnp.float32),
            pltpu.VMEM((4, chips, rows, half), jnp.float32),
            pltpu.VMEM((4, chips - 1, rows, half), jnp.float32),
            pltpu.VMEM((rows, half), jnp.float32),
            dma((4, chips)), dma((4, chips)), dma((4, chips)),
            dma((4, chips - 1)), dma((4, chips - 1)),
            dma, dma,
        ],
        compiler_params=pltpu.CompilerParams(
            collective_id=0, has_side_effects=True, vmem_limit_bytes=60 * 2**20
        ),
    )(window.reshape(2, n_col, rows, width))


def on_device(interior_factor, coupling_in, coupling_back, interface_block, gran_count, gran_index):
    n_row, n_col = lax.axis_size("row"), lax.axis_size("col")
    r, c = lax.axis_index("row"), lax.axis_index("col")
    window = None
    for member in range(gran_count.shape[2]):
        count = gran_count[r, c, member]
        index = gran_index[r, c, member]
        slots = jnp.arange(index.shape[0], dtype=jnp.int32)
        slot = jnp.sum(jnp.where(index[:, None] == slots[None, :], slots[:, None], 0), axis=0, dtype=jnp.int32)
        live = (slot < count).astype(jnp.int32)
        part = assemble(
            slot, live, interior_factor[0, 0, member], coupling_in[0, 0, member],
            coupling_back[0, 0, member], interface_block[0, 0, member],
        )
        window = part if window is None else window + part
    return exchange(window, n_row, n_col)[None]


def solution(mesh):
    spec = P("row", "col", None, None, None)
    return jax.shard_map(
        on_device, mesh=mesh, in_specs=(spec, spec, spec, spec, P(), P()),
        out_specs=P("row", None, "col", None), check_vma=False,
    )
```

time: 956 us -> 142 us (0.15); the launches traced: 942 us -> 140 us
  waiting for transfers between devices: 723 us -> 0 us
  Pallas kernels: 0 us -> 127 us
  other arithmetic: 85.8 us -> 0.74 us
  matrix products: 65.5 us -> 0 us
  local copies, waits for them, and re-layouts: 49.1 us -> 12.5 us
  between operations: 16.5 us -> 0.03 us
    reduce_scatter x1 -> x0, waiting for transfers between devices: 697 us -> none  [on_device(): summed = lax.psum_scatter(quarters, 'col', scatter_dimension=1, tiled=True)]
    pallas_call x0 -> x2, Pallas kernels: none -> 127 us  [the longest x1 101 us: exchange(): pl.pallas_call(functools.partial(exchange_kernel, n_row, n_col), out_shap...]
    another operation x10 -> x0, other arithmetic: 72 us -> none  [the longest x8 61.2 us: solve_block(): lax.linalg.triangular_solve(factor, piece, left_side=True, lower=True)]
    dot_general x3 -> x0, matrix products: 62.5 us -> none  [the longest x2 59.6 us: place(): jnp.einsum('ap,aibj,bq->piqj', table, blocks, table, precision=lax.Precis...]
    ppermute x1 -> x0, waiting for transfers between devices: 26 us -> none  [from_behind(): return lax.ppermute(block, axis, route)]
    another operation x23 -> x0, local copies, waits for them, and re-layouts: 17 us -> none  [the longest x20 11.9 us: solve_block(): lax.linalg.triangular_solve(factor, piece, left_side=True, lower=True)]
  transfers between devices with their start and end apart: 2 -> 0, of which waited for: 2 -> 0; matrix products, arithmetic and copies ran while one was open for 0% -> 0% of each run, Pallas kernels for 0% -> 0%
where the time goes in v1:
time: 142 us; the launch traced here: 140 us
  Pallas kernels  127 us (89%)
  local copies, waits for them, and re-layouts  12.5 us (9%)
    pallas_call x1, Pallas kernels, exchange(): pl.pallas_call(functools.partial(exchange_kernel, n_row, n_col), out_shap...  101 us
    pallas_call x1, Pallas kernels, assemble(): pl.pallas_call(functools.partial(assemble_kernel, granule, tile), grid_sp...  25.4 us
    unnamed x11, local copies, waits for them, and re-layouts  11.2 us

profile of v1, /device:TPU:0, one launch (start us, length us, event | category | flops | bytes accessed | tf_op | source)
XLA Modules:
  0.0 139.9 jit_solution(9317704551450955886)
XLA Ops:
  0.0 0.0 copy-start
  0.0 1.2 constant_dynamic-slice_fusion
  1.3 0.0 copy-done
  1.3 0.1 select_reduce_fusion.slot_ref
  1.3 0.6 compare_convert_fusion.live_ref
  2.0 0.0 copy-start.1
  2.0 3.4 %copy-done.1 = bf16[1,1,1,2048,2048]{4,3,2,1,0:T(8,128)(2,1)S(1)} copy-done((bf16[1,1,1,2048,2048]{4,3,2,1,0:T(8,128)(2,1)S(1)}, bf16[1,1,1,2048,2048]{4,3,2,1,0:T(8,128)(2,1)}, u32[]{:S(2)}) %copy-start.1) | copy-done | bytes 8388632
  5.4 0.0 copy-start.2
  5.4 1.4 %copy-done.2 = bf16[1,1,1,384,2048]{4,3,2,1,0:T(8,128)(2,1)S(1)} copy-done((bf16[1,1,1,384,2048]{4,3,2,1,0:T(8,128)(2,1)S(1)}, bf16[1,1,1,384,2048]{4,3,2,1,0:T(8,128)(2,1)}, u32[]{:S(2)}) %copy-start.2) | copy-done | bytes 1572888
  6.8 0.0 copy-start.3
  6.8 1.4 %copy-done.3 = bf16[1,1,1,384,2048]{4,3,2,1,0:T(8,128)(2,1)S(1)} copy-done((bf16[1,1,1,384,2048]{4,3,2,1,0:T(8,128)(2,1)S(1)}, bf16[1,1,1,384,2048]{4,3,2,1,0:T(8,128)(2,1)}, u32[]{:S(2)}) %copy-start.3) | copy-done | bytes 1572888
  8.2 0.0 copy-start.4
  8.2 1.1 copy-done.4
  9.3 25.4 %shard_map.64 = f32[2048,2048]{1,0:T(8,128)} custom-call(s32[16]{0:T(128)S(1)} %select_reduce_fusion.slot_ref, s32[16]{0:T(128)S(1)} %compare_convert_fusion.live_ref, f32[384,384]{1,0:T(8,128)S(1)} %bitcast.12, bf16[384,2048]{1,0:T(8,128)(2,1)S(1)} %bitcast.10, bf16[384,2048]{1,0:T(8,128)(2,1)S(1)} %bitcast.11, bf16[2048,2048]{1,0:T(8,128)(2,1)S(1)} %bitcast.9), custom_call_target="tpu_custom_call" | custom-call | tf_op jit(solution)/shard_map/pallas_call | solution.py:105
  34.7 101.2 %shard_map.65 = f32[3,256,1024]{2,1,0:T(8,128)} custom-call(f32[2,4,256,2048]{3,2,1,0:T(8,128)} %bitcast.13), custom_call_target="tpu_custom_call" | custom-call | tf_op jit(solution)/shard_map/pallas_call | solution.py:209
  135.9 4.0 %copy.8 = f32[1,3,256,1024]{3,2,1,0:T(8,128)} copy(f32[1,3,256,1024]{3,2,1,0:T(8,128)} %bitcast.14) | data formatting | bytes 6291456
  (1 shorter events, 0.0 us)
Async XLA Ops:
  0.0 1.3 copy-start
  2.0 3.4 %copy-start.1 = (bf16[1,1,1,2048,2048]{4,3,2,1,0:T(8,128)(2,1)S(1)}, bf16[1,1,1,2048,2048]{4,3,2,1,0:T(8,128)(2,1)}, u32[]{:S(2)}) copy-start(bf16[1,1,1,2048,2048]{4,3,2,1,0:T(8,128)(2,1)} %param.9) | copy-start | bytes 25165828
  5.4 1.4 %copy-start.2 = (bf16[1,1,1,384,2048]{4,3,2,1,0:T(8,128)(2,1)S(1)}, bf16[1,1,1,384,2048]{4,3,2,1,0:T(8,128)(2,1)}, u32[]{:S(2)}) copy-start(bf16[1,1,1,384,2048]{4,3,2,1,0:T(8,128)(2,1)} %param.7) | copy-start | bytes 4718596
  6.8 1.4 %copy-start.3 = (bf16[1,1,1,384,2048]{4,3,2,1,0:T(8,128)(2,1)S(1)}, bf16[1,1,1,384,2048]{4,3,2,1,0:T(8,128)(2,1)}, u32[]{:S(2)}) copy-start(bf16[1,1,1,384,2048]{4,3,2,1,0:T(8,128)(2,1)} %param.8) | copy-start | bytes 4718596
  8.2 1.1 copy-start.4

commit v2 on v1

--- a/solution.py
+++ b/solution.py
@@ -118,14 +118,35 @@
             + [pltpu.VMEM((ni, width), jnp.bfloat16)] * 2,
         ),
         out_shape=jax.ShapeDtypeStruct((width, width), jnp.float32),
-        compiler_params=pltpu.CompilerParams(vmem_limit_bytes=40 * 2**20),
+        compiler_params=pltpu.CompilerParams(vmem_limit_bytes=60 * 2**20),
     )(slot, live, factor, inner, back, own)
+
+
+LEVELS = 32767.0
+
+
+def encode(values, group):
+    codes, sizes = [], []
+    for first in range(0, values.shape[0], group):
+        part = values[first:first + group]
+        size = jnp.maximum(jnp.max(jnp.abs(part), axis=0, keepdims=True), 1e-33)
+        codes.append(jnp.round(part * (LEVELS / size)).astype(jnp.int32).astype(jnp.int16))
+        sizes.append(size)
+    return codes, sizes
+
+
+def decode(code_ref, size_ref, at, group):
+    parts = []
+    for g in range(code_ref.shape[-2] // group):
+        code = code_ref[at + (pl.ds(g * group, group),)].astype(jnp.int32).astype(jnp.float32)
+        parts.append(code * (size_ref[at + (pl.ds(g, 1),)] * (1.0 / LEVELS)))
+    return parts[0] if len(parts) == 1 else jnp.concatenate(parts, axis=0)
 
 
 def exchange_kernel(
     n_row, n_col, w_ref, out_ref,
-    mine, paired, arrived, carried,
-    load_sem, send1, recv1, send2, recv2, send3, recv3,
+    mine, paired, codes, sizes, arrived, arrived_sizes, carried,
+    load_sem, send1, recv1, send2, recv2, send_size, recv_size, send3, recv3,
 ):
     chips = n_col // 2
     rows, half = mine.shape[2], mine.shape[3]
@@ -149,7 +170,8 @@
         device = lax.rem(chip + o, chips) * 2 + which
         return w_ref.at[q // 2, device, :, pl.ds((q % 2) * half, half)]
 
-    loads, first, second = {}, {}, {}
+    group = min(128, rows)
+    loads, first, second, second_size = {}, {}, {}, {}
     for q in order:
         for o in offsets:
             loads[q, o] = pltpu.make_async_copy(part(q, o, core), mine.at[q, o], load_sem.at[q, o])
@@ -167,15 +189,26 @@
         for o in offsets:
             loads[q, o].wait()
             first[q, o].wait_recv()
-            mine[q, o] = mine[q, o] + paired[q, o]
-            if o:
+            if not o:
+                mine[q, o] = mine[q, o] + paired[q, o]
+            else:
+                new_codes, new_sizes = encode(mine[q, o] + paired[q, o], group)
+                for g in range(len(new_codes)):
+                    codes[q, o - 1, pl.ds(g * group, group)] = new_codes[g]
+                    sizes[q, o - 1, pl.ds(g, 1)] = new_sizes[g]
                 device = lax.rem(chip + o, chips) * 2 + core
                 second[q, o] = pltpu.make_async_remote_copy(
-                    src_ref=mine.at[q, o], dst_ref=arrived.at[q, o - 1],
+                    src_ref=codes.at[q, o - 1], dst_ref=arrived.at[q, o - 1],
                     send_sem=send2.at[q, o - 1], recv_sem=recv2.at[q, o - 1],
                     device_id=(r, device), device_id_type=MESH,
                 )
                 second[q, o].start()
+                second_size[q, o] = pltpu.make_async_remote_copy(
+                    src_ref=sizes.at[q, o - 1], dst_ref=arrived_sizes.at[q, o - 1],
+                    send_sem=send_size.at[q, o - 1], recv_sem=recv_size.at[q, o - 1],
+                    device_id=(r, device), device_id_type=MESH,
+                )
+                second_size[q, o].start()
     carry = pltpu.make_async_remote_copy(
         src_ref=mine.at[3, 0], dst_ref=carried, send_sem=send3, recv_sem=recv3,
         device_id=(after, c), device_id_type=MESH,
@@ -184,7 +217,8 @@
         total = mine[q, 0]
         for o in range(1, chips):
             second[q, o].wait_recv()
-            total = total + arrived[q, o - 1]
+            second_size[q, o].wait_recv()
+            total = total + decode(arrived, arrived_sizes, (q, o - 1), group)
         if q == 3:
             mine[q, 0] = total
             carry.start()
@@ -195,7 +229,7 @@
             out_ref[q] = total + carried[...]
     for copy in first.values():
         copy.wait_send()
-    for copy in second.values():
+    for copy in [*second.values(), *second_size.values()]:
         copy.wait_send()
     carry.wait_send()
 
@@ -205,6 +239,7 @@
     half = width // 2
     rows = half // n_col
     chips = n_col // 2
+    groups = rows // min(128, rows)
     dma = pltpu.SemaphoreType.DMA
     return pl.pallas_call(
         functools.partial(exchange_kernel, n_row, n_col),
@@ -214,9 +249,13 @@
         scratch_shapes=[
             pltpu.VMEM((4, chips, rows, half), jnp.float32),
             pltpu.VMEM((4, chips, rows, half), jnp.float32),
-            pltpu.VMEM((4, chips - 1, rows, half), jnp.float32),
+            pltpu.VMEM((4, chips - 1, rows, half), jnp.int16),
+            pltpu.VMEM((4, chips - 1, groups, half), jnp.float32),
+            pltpu.VMEM((4, chips - 1, rows, half), jnp.int16),
+            pltpu.VMEM((4, chips - 1, groups, half), jnp.float32),
             pltpu.VMEM((rows, half), jnp.float32),
             dma((4, chips)), dma((4, chips)), dma((4, chips)),
+            dma((4, chips - 1)), dma((4, chips - 1)),
             dma((4, chips - 1)), dma((4, chips - 1)),
             dma, dma,
         ],

time: 142 us -> 97.2 us (0.68)
  Pallas kernels: 127 us -> 89.3 us
  local copies, waits for them, and re-layouts: 12.5 us -> 5.31 us
    pallas_call x1, Pallas kernels: 101 us -> 57.3 us  [exchange(): pl.pallas_call(functools.partial(exchange_kernel, n_row, n_col), out_shap...]
    unnamed x11 -> x5, local copies, waits for them, and re-layouts: 11.2 us -> 3.98 us
    pallas_call x1, Pallas kernels: 25.4 us -> 32 us  [assemble(): pl.pallas_call(functools.partial(assemble_kernel, granule, tile), grid_sp...]
where the time goes in v2:
time: 97.2 us; the launch traced here: 95.9 us
  Pallas kernels  89.3 us (92%)
  local copies, waits for them, and re-layouts  5.31 us (5%)
  other arithmetic  1.29 us (1%)
    pallas_call x1, Pallas kernels, exchange(): pl.pallas_call(functools.partial(exchange_kernel, n_row, n_col), out_shap...  57.3 us
    pallas_call x1, Pallas kernels, assemble(): pl.pallas_call(functools.partial(assemble_kernel, granule, tile), grid_sp...  32 us
    unnamed x5, local copies, waits for them, and re-layouts  3.98 us

profile of v2, /device:TPU:0, one launch (start us, length us, event | category | flops | bytes accessed | tf_op | source)
XLA Modules:
  0.0 95.9 jit_solution(15114316723094317815)
XLA Ops:
  0.0 0.0 copy-start
  0.0 1.3 %constant_dynamic-slice_fusion = s32[1,1,1]{0,2,1:T(1,128)} fusion(s32[8,4,1]{0,2,1:T(1,128)} %param.10, s32[]{:T(128)S(6)} %select_n.12, s32[]{:T(128)S(6)} %select_n.13), kind=kLoop, calls=%fused_computation.4 | loop fusion | bytes 16 | tf_op jit(solution)/shard_map/dynamic_slice | solution.py:273
  1.3 0.0 copy-done
  1.3 0.1 select_reduce_fusion.slot_ref
  1.4 0.0 copy-start.1
  1.4 1.2 %compare_convert_fusion.live_ref = s32[16]{0:T(128)} fusion(s32[16]{0:T(128)S(1)} %select_reduce_fusion.slot_ref, s32[]{:T(128)} %bitcast.1), kind=kLoop, calls=%fused_computation.2 | loop fusion | flops 32 | bytes 132 | tf_op jit(solution)/shard_map/convert_element_type | solution.py:277
  2.6 0.0 copy-done.1
  2.6 32.0 %shard_map.64 = f32[2048,2048]{1,0:T(8,128)} custom-call(s32[16]{0:T(128)} %copy-done.1, s32[16]{0:T(128)} %compare_convert_fusion.live_ref, f32[384,384]{1,0:T(8,128)} %bitcast.14, bf16[384,2048]{1,0:T(8,128)(2,1)} %bitcast.12, bf16[384,2048]{1,0:T(8,128)(2,1)} %bitcast.13, bf16[2048,2048]{1,0:T(8,128)(2,1)} %bitcast.11), custom_call_target="tpu_custom_call" | custom-call | tf_op jit(solution)/shard_map/pallas_call | solution.py:105
  34.6 57.3 %shard_map.65 = f32[3,256,1024]{2,1,0:T(8,128)} custom-call(f32[2,4,256,2048]{3,2,1,0:T(8,128)} %bitcast.9), custom_call_target="tpu_custom_call" | custom-call | tf_op jit(solution)/shard_map/pallas_call | solution.py:244
  91.9 4.0 %copy.8 = f32[1,3,256,1024]{3,2,1,0:T(8,128)} copy(f32[1,3,256,1024]{3,2,1,0:T(8,128)} %bitcast.10) | data formatting | bytes 6291456
  (1 shorter events, 0.0 us)
Async XLA Ops:
  0.0 1.3 %copy-start = (s32[8,4,1,16]{3,2,1,0:T(1,128)S(1)}, s32[8,4,1,16]{3,2,1,0:T(1,128)}, u32[]{:S(2)}) copy-start(s32[8,4,1,16]{3,2,1,0:T(1,128)} %param.11) | copy-start | bytes 6148
  1.4 1.2 %copy-start.1 = (s32[16]{0:T(128)}, s32[16]{0:T(128)S(1)}, u32[]{:S(2)}) copy-start(s32[16]{0:T(128)S(1)} %select_reduce_fusion.slot_ref) | copy-start | bytes 196
